TPU v7x, 32 devices: a whole 2x2x4 slice. The times are simulated.
32 devices in a mesh: row: 4 (over y, x), col: 8 (over z, core).
Axes of the slice: x: 2, y: 2, z: 4, core: 2. Of those that a mesh axis runs over, the one named last changes fastest.
Arguments:
- vorticity: float32 [3, 128, 128, 128], P(None, 'row', 'col'), may hold values from -18.1 to 18.1
- scalar: float32 [256, 256, 256], P('row', 'col'), may hold values from -6 to 6
Outputs:
- advected: float32 [256, 256, 256], P('row', 'col')
All inputs are finite; a program needn't handle non-finite values. Where the computation divides by a largest or mean magnitude, that divisor is 1e-20 or more.
Results may differ from a plain program's by a relative error of at most 0.0003.
Values sent between devices are 32-bit elements; how exact they have to be, the bound alone decides.
A program may use at most 128 MiB of HBM per device.

v0:
```python
import math
import jax
import jax.numpy as jnp
from jax import lax
from jax.sharding import PartitionSpec as P

COURANT = 0.9
EPSILON = 1e-06
HIGHEST = lax.Precision.HIGHEST


def with_halo(cells, sides, width):
    for axis, dim in sides:
        count = lax.axis_size(axis)
        head = lax.slice_in_dim(cells, 0, width, axis=dim)
        tail = lax.slice_in_dim(cells, cells.shape[dim] - width, cells.shape[dim], axis=dim)
        cells = jnp.concatenate(
            [
                lax.ppermute(tail, axis, [(i, (i + 1) % count) for i in range(count)]),
                cells,
                lax.ppermute(head, axis, [((i + 1) % count, i) for i in range(count)]),
            ],
            axis=dim,
        )
    return cells


def kernel_weight(distance):
    radius = jnp.abs(distance)
    inner_lobe = (
        -(radius - 1.0)
        * ((((25.0 * radius - 38.0) * radius - 3.0) * radius + 12.0) * radius + 12.0)
        / 12.0
    )
    middle_lobe = (
        (radius - 1.0)
        * (radius - 2.0)
        * (((25.0 * radius - 114.0) * radius + 153.0) * radius - 48.0)
        / 24.0
    )
    outer_cube = (radius - 3.0) * (radius - 3.0) * (radius - 3.0)
    outer_lobe = -(radius - 2.0) * outer_cube * (5.0 * radius - 8.0) / 24.0
    return jnp.where(
        radius < 1.0,
        inner_lobe,
        jnp.where(radius < 2.0, middle_lobe, jnp.where(radius < 3.0, outer_lobe, 0.0)),
    )


def tables(length):
    indices = jnp.arange(length, dtype=jnp.int32)
    product = indices[:, None] * indices[None, :] % length
    angle = product.astype(jnp.float32) * (2.0 * math.pi / length)
    return (jnp.cos(angle), jnp.sin(angle))


def rotate(complex_pair, formula, cosine, sine, direction):
    real_cos = jnp.einsum(formula, complex_pair[0], cosine, precision=HIGHEST)
    real_sin = jnp.einsum(formula, complex_pair[0], sine, precision=HIGHEST)
    imag_cos = jnp.einsum(formula, complex_pair[1], cosine, precision=HIGHEST)
    imag_sin = jnp.einsum(formula, complex_pair[1], sine, precision=HIGHEST)
    return jnp.stack([real_cos - direction * imag_sin, imag_cos + direction * real_sin])


def wavenumber(start, count, length):
    indices = start + jnp.arange(count, dtype=jnp.int32)
    waves = jnp.where(indices < length // 2, indices, indices - length).astype(jnp.float32)
    return (waves, indices == length // 2)


def induce(spectrum, xwaves, ywaves, zwaves, banned, inverse_cube):
    wave_sq = xwaves * xwaves + ywaves * ywaves + zwaves * zwaves
    keep = (wave_sq > 0.0) & jnp.logical_not(banned)
    factor = jnp.where(keep, 1.0 / jnp.maximum(wave_sq, 1.0), 0.0) * inverse_cube
    crosses = []
    for part_index in range(2):
        omega = spectrum[part_index]
        crosses.append(
            jnp.stack(
                [
                    ywaves * omega[2] - zwaves * omega[1],
                    zwaves * omega[0] - xwaves * omega[2],
                    xwaves * omega[1] - ywaves * omega[0],
                ]
            )
        )
    return jnp.stack([-crosses[1] * factor, crosses[0] * factor])


def merged_shape(lower, grid_axis):
    shape = list(lower.shape)
    shape[grid_axis] = 2 * shape[grid_axis]
    return shape


def refine_roll(coarse, grid_axis):
    lower = 0.75 * coarse + 0.25 * jnp.roll(coarse, 1, grid_axis)
    upper = 0.75 * coarse + 0.25 * jnp.roll(coarse, -1, grid_axis)
    return jnp.stack([lower, upper], axis=grid_axis + 1).reshape(merged_shape(lower, grid_axis))


def refine_rim(coarse, grid_axis):
    length = coarse.shape[grid_axis]
    inner = lax.slice_in_dim(coarse, 1, length - 1, axis=grid_axis)
    below = lax.slice_in_dim(coarse, 0, length - 2, axis=grid_axis)
    above = lax.slice_in_dim(coarse, 2, length, axis=grid_axis)
    lower = 0.75 * inner + 0.25 * below
    upper = 0.75 * inner + 0.25 * above
    return jnp.stack([lower, upper], axis=grid_axis + 1).reshape(merged_shape(lower, grid_axis))


def remesh_roll(field, displace, grid_axis):
    summed = jnp.zeros(field.shape, jnp.float32)
    for offset in range(-3, 4):
        summed = summed + jnp.roll(field, offset, grid_axis) * kernel_weight(
            offset - jnp.roll(displace, offset, grid_axis)
        )
    return summed


def remesh_rim(field_ext, displace_ext, grid_axis, count):
    shape = list(field_ext.shape)
    shape[grid_axis] = count
    summed = jnp.zeros(shape, jnp.float32)
    for offset in range(-3, 4):
        begin = 3 - offset
        values = lax.slice_in_dim(field_ext, begin, begin + count, axis=grid_axis)
        moved = lax.slice_in_dim(displace_ext, begin, begin + count, axis=grid_axis)
        summed = summed + values * kernel_weight(offset - moved)
    return summed


def shards(vorticity, scalar):
    coarse_n = vorticity.shape[3]
    cos_full, sin_full = tables(coarse_n)
    mode_count = coarse_n // 2
    weights = jnp.where(jnp.arange(mode_count) == 0, 1.0, 2.0).astype(jnp.float32)
    cos_fwd = cos_full[:, :mode_count]
    sin_fwd = sin_full[:, :mode_count]
    cos_back = cos_full[:mode_count, :] * weights[:, None]
    sin_back = sin_full[:mode_count, :] * weights[:, None]
    forward = jnp.stack(
        [
            jnp.einsum("cyzx,xk->cyzk", vorticity, cos_fwd, precision=HIGHEST),
            -jnp.einsum("cyzx,xk->cyzk", vorticity, sin_fwd, precision=HIGHEST),
        ]
    )
    spectrum = rotate(
        lax.all_to_all(forward, "row", split_axis=4, concat_axis=2, tiled=True),
        "cyzk,yq->czkq",
        cos_full,
        sin_full,
        -1.0,
    )
    spectrum = rotate(
        lax.all_to_all(spectrum, "col", split_axis=4, concat_axis=2, tiled=True),
        "czkq,zw->ckqw",
        cos_full,
        sin_full,
        -1.0,
    )
    first_count = spectrum.shape[2]
    second_count = spectrum.shape[3]
    xwaves, xnyquist = wavenumber(lax.axis_index("row") * first_count, first_count, coarse_n)
    ywaves, ynyquist = wavenumber(lax.axis_index("col") * second_count, second_count, coarse_n)
    zwaves, znyquist = wavenumber(0, coarse_n, coarse_n)
    banned = xnyquist[:, None, None] | ynyquist[None, :, None] | znyquist[None, None, :]
    inverse_cube = 1.0 / (coarse_n * coarse_n * coarse_n)
    velocity_hat = induce(
        spectrum,
        xwaves[:, None, None],
        ywaves[None, :, None],
        zwaves[None, None, :],
        banned,
        inverse_cube,
    )
    inverse_z = rotate(velocity_hat, "ckqw,wz->ckqz", cos_full, sin_full, 1.0)
    mixed = rotate(
        lax.all_to_all(inverse_z, "col", split_axis=4, concat_axis=3, tiled=True),
        "ckqz,qy->ckzy",
        cos_full,
        sin_full,
        1.0,
    )
    block = lax.all_to_all(mixed, "row", split_axis=4, concat_axis=2, tiled=True)
    velocity = jnp.einsum("ckzy,kx->cyzx", block[0], cos_back, precision=HIGHEST) - jnp.einsum(
        "ckzy,kx->cyzx", block[1], sin_back, precision=HIGHEST
    )
    velocity_peak = lax.pmax(jnp.max(jnp.abs(velocity)), ("row", "col"))
    courant_scale = COURANT / (velocity_peak + EPSILON)
    fine_rows = scalar.shape[0]
    fine_cols = scalar.shape[1]
    rimmed = with_halo(velocity, (("row", 1), ("col", 2)), 1)
    displaced = refine_rim(refine_rim(refine_roll(rimmed, 3), 1), 2) * courant_scale
    swept = remesh_roll(scalar, displaced[0], 2)
    rows_input = jnp.stack([swept, displaced[1]])
    rows_ext = with_halo(rows_input, (("row", 1),), 3)
    ymoved = rows_ext[1]
    swept = remesh_rim(rows_ext[0], ymoved, 0, fine_rows)
    cols_input = jnp.stack([swept, displaced[2]])
    cols_ext = with_halo(cols_input, (("col", 2),), 3)
    zmoved = cols_ext[1]
    return remesh_rim(cols_ext[0], zmoved, 1, fine_cols)


def solution(mesh):
    in_specs = (P(None, "row", "col", None), P("row", "col", None))
    out_specs = P("row", "col", None)
    return jax.shard_map(shards, mesh=mesh, in_specs=in_specs, out_specs=out_specs, check_vma=False)
```

profile of v0, /device:TPU:1, one launch (start us, length us, event | category | flops | bytes accessed | tf_op | source)
XLA Modules:
  0.0 478.1 jit_solution(8644423327381944516)
XLA Ops:
  9.0 14.5 %all_to_all.60 = f32[4,1,49152]{2,1,0:T(1,128)S(1)} all-to-all(f32[4,1,49152]{2,1,0:T(1,128)S(1)} %reshape.296), channel_id=1, replica_groups=mesh['row'=4,'col'=8] {'row'}, dimensions={0} | all-to-all | bytes 1572864 | tf_op jit(solution)/shard_map/all_to_all | solution.py:149
  44.6 6.5 %copy.296 = f32[2,3,16,16,128]{3,2,1,0,4:T(8,128)} copy(f32[2,3,16,16,128]{4,3,2,1,0:T(8,128)S(1)} %pad_maximum_fusion.7) | data formatting | bytes 1572864 | tf_op jit(solution)/shard_map/stack | solution.py:62
  56.6 7.0 %all-to-all-start.1 = ((f32[8,1,24576]{2,1,0:T(1,128)}), f32[8,1,24576]{2,1,0:T(1,128)S(1)}, u32[]{:S(2)}, u32[]{:S(2)}) async-start(f32[8,1,24576]{2,1,0:T(1,128)} %reshape.298), calls=%async_computation.1 | async-start | bytes 1572864 | tf_op jit(solution)/shard_map/all_to_all | solution.py:156
  64.0 19.6 %all-to-all-done.1 = f32[8,1,24576]{2,1,0:T(1,128)S(1)} async-done(((f32[8,1,24576]{2,1,0:T(1,128)}), f32[8,1,24576]{2,1,0:T(1,128)S(1)}, u32[]{:S(2)}, u32[]{:S(2)}) %all-to-all-start.1) | async-done | bytes 786464 | tf_op jit(solution)/shard_map/all_to_all | solution.py:156
  91.0 8.0 %copy.297 = f32[2,3,16,16,8,16]{2,4,5,3,1,0:T(8,128)} copy(f32[2,3,16,16,8,16]{3,2,1,0,5,4:T(8,128)} %bitcast.182) | data formatting | bytes 1572864 | tf_op jit(solution)/shard_map/all_to_all | solution.py:156
  99.0 6.3 %fusion.342 = (f32[1,3,8,16,16,16]{3,2,5,4,1,0:T(8,128)}, f32[1,3,8,16,16,16]{3,2,5,4,1,0:T(8,128)}) fusion(f32[2,3,8,16,16,16]{3,2,5,4,1,0:T(8,128)} %bitcast.179), kind=kLoop, calls=%fused_computation.442 | loop fusion | bytes 1572864 | tf_op jit(solution)/shard_map/slice | solution.py:59
  116.4 6.0 %copy.298 = f32[2,3,16,16,128]{3,2,1,0,4:T(8,128)} copy(f32[2,3,16,16,128]{4,3,2,1,0:T(8,128)S(1)} %pad_maximum_fusion.8) | data formatting | bytes 1572864 | tf_op jit(solution)/shard_map/stack | solution.py:62
  122.4 5.6 %reshape.300 = f32[8,1,24576]{2,1,0:T(1,128)} reshape(f32[128,2,3,16,16]{4,3,2,1,0:T(8,128)} %bitcast.183) | data formatting | bytes 1572864
  139.1 14.3 %all-to-all-done.2 = f32[8,1,24576]{2,1,0:T(1,128)} async-done(((f32[8,1,24576]{2,1,0:T(1,128)}), f32[8,1,24576]{2,1,0:T(1,128)}, u32[]{:S(2)}, u32[]{:S(2)}) %all-to-all-start.2) | async-done | bytes 786464 | tf_op jit(solution)/shard_map/all_to_all | solution.py:179
  161.9 6.4 %copy.353 = f32[2,3,16,16,8,16]{3,4,5,2,1,0:T(8,128)S(1)} copy(f32[2,3,16,16,8,16]{3,2,1,0,5,4:T(8,128)} %bitcast.184) | data formatting | bytes 1572864 | tf_op jit(solution)/shard_map/all_to_all | solution.py:179
  179.7 6.0 %copy.300 = f32[2,3,16,16,128]{3,2,1,0,4:T(8,128)} copy(f32[2,3,16,16,128]{4,3,2,1,0:T(8,128)S(1)} %pad_maximum_fusion.9) | data formatting | bytes 1572864 | tf_op jit(solution)/shard_map/stack | solution.py:62
  199.9 5.9 %all-to-all-done.3 = f32[4,1,49152]{2,1,0:T(1,128)} async-done(((f32[4,1,49152]{2,1,0:T(1,128)}), f32[4,1,49152]{2,1,0:T(1,128)}, u32[]{:S(2)}, u32[]{:S(2)}) %all-to-all-start.3) | async-done | bytes 786464 | tf_op jit(solution)/shard_map/all_to_all | solution.py:185
  214.5 6.7 %copy.301 = f32[2,3,16,16,4,32]{5,3,2,4,1,0:T(8,128)} copy(f32[2,3,16,16,4,32]{3,2,1,0,5,4:T(8,128)} %bitcast.186) | data formatting | bytes 1572864 | tf_op jit(solution)/shard_map/all_to_all | solution.py:185
  267.1 40.1 %pmax.7 = f32[]{:T(128)} all-reduce(f32[]{:T(128)} %get-tuple-element.5), channel_id=1, replica_groups=mesh['row'=4,'col'=8] {'row','col'}, use_global_device_ids=true, to_apply=%region_1.2 | all-reduce | flops 1 | bytes 8 | tf_op jit(solution)/shard_map/pmax | solution.py:189
  312.0 9.8 %copy.310 = f32[3,34,18,128,2]{1,4,3,2,0:T(2,128)} copy(f32[3,34,18,128,2]{3,1,2,0,4:T(8,128)} %pad_maximum_fusion.3) | data formatting | bytes 3760128 | tf_op jit(solution)/shard_map/stack | solution.py:99
  321.8 12.1 %fusion.3 = (f32[3,32,1,18,256]{1,4,3,0,2:T(8,128)}, f32[3,32,1,18,256]{1,4,3,0,2:T(8,128)}) fusion(f32[3,34,18,256]{1,3,2,0:T(8,128)} %bitcast.175), kind=kLoop, calls=%fused_computation.6 | loop fusion | flops 2211840 | bytes 8847360 | tf_op jit(solution)/shard_map/stack | solution.py:109
  333.9 12.6 %pad_maximum_fusion = f32[3,32,2,18,256]{1,4,3,0,2:T(8,128)} fusion(f32[3,32,1,18,256]{1,4,3,0,2:T(8,128)} %get-tuple-element.8, f32[3,32,1,18,256]{1,4,3,0,2:T(8,128)} %get-tuple-element.7), kind=kLoop, calls=%fused_computation | loop fusion | flops 884736 | bytes 7077888 | tf_op jit(solution)/shard_map/stack | solution.py:109
  346.5 11.0 %copy.311 = f32[3,32,2,18,256]{4,2,1,3,0:T(2,128)} copy(f32[3,32,2,18,256]{1,4,3,0,2:T(8,128)} %pad_maximum_fusion) | data formatting | bytes 7077888 | tf_op jit(solution)/shard_map/stack | solution.py:109
  357.5 5.8 %reshape.287 = f32[3,64,18,256]{3,1,2,0:T(8,128)} reshape(f32[3,32,2,18,256]{4,2,1,3,0:T(2,128)} %copy.311) | data formatting | bytes 7077888 | tf_op jit(solution)/shard_map/reshape | solution.py:109
  380.5 23.9 %fusion.21 = f32[1,64,32,256]{3,1,2,0:T(8,128)S(1)} fusion(f32[64,32,3]{2,0,1:T(8,128)S(1)} %copy-done.15, f32[64,32,253]{2,0,1:T(8,128)S(1)} %copy-done.9, f32[64,32,2]{2,0,1:T(8,128)S(1)} %copy-done.16, f32[64,32,254]{2,0,1:T(8,128)S(1)} %copy-done.10, f32[64,32,1]{2,0,1:T(8,128)S(1)} %copy-done.17, f32[64,32,255]{2,0,1:T(8,128)S(1)} %copy-done.11, ...), kind=kLoop, calls=%fused_computation.57 | loop fusion | flops 152567808 | bytes 31457280 | tf_op jit(solution)/shard_map/stack | solution.py:196
  412.0 6.3 %collective-permute-done.5 = f32[2,3,32,256]{3,1,2,0:T(4,128)S(1)} collective-permute-done((f32[2,3,32,256]{3,1,2,0:T(4,128)S(1)}, f32[2,3,32,256]{3,1,2,0:T(4,128)S(1)}, u32[]{:S(2)}, u32[]{:S(2)}) %collective-permute-start.5) | collective-permute-done | bytes 196640 | tf_op jit(solution)/shard_map/ppermute | solution.py:19
  419.8 20.3 %fusion.76 = f32[1,64,32,256]{3,1,2,0:T(8,128)S(1)} fusion(f32[1,64,32,256]{3,1,2,0:T(8,128)S(1)} %fusion.21, f32[2,67,32,256]{3,1,2,0:T(8,128)S(1)} %get-tuple-element.21, f32[2,67,32,256]{3,1,2,0:T(8,128)S(1)} %get-tuple-element.20, f32[1,64,32,256]{3,1,2,0:T(8,128)S(1)} %bitcast.178), kind=kLoop, calls=%fused_computation.112 | loop fusion | flops 146276352 | bytes 31457280 | tf_op jit(solution)/shard_map/add | solution.py:129
  445.0 7.7 %collective-permute-done.6 = f32[2,64,3,256]{3,1,2,0:T(8,128)S(1)} collective-permute-done((f32[2,64,3,256]{3,1,2,0:T(8,128)S(1)}, f32[2,64,3,256]{3,1,2,0:T(8,128)S(1)}, u32[]{:S(2)}, u32[]{:S(2)}) %collective-permute-start.6) | collective-permute-done | bytes 393248 | tf_op jit(solution)/shard_map/ppermute | solution.py:19
  456.4 19.0 %fusion.131 = f32[64,32,256]{2,0,1:T(8,128)S(1)} fusion(f32[64,38,256]{2,0,1:T(8,128)S(1)} %get-tuple-element.17, f32[64,38,256]{2,0,1:T(8,128)S(1)} %get-tuple-element.16), kind=kLoop, calls=%fused_computation.167 | loop fusion | flops 146276352 | bytes 31457280 | tf_op jit(solution)/shard_map/add | solution.py:129
  (173 shorter events, 194.9 us)
Async XLA Ops:
  56.6 27.0 %all-to-all-start.1 = ((f32[8,1,24576]{2,1,0:T(1,128)}), f32[8,1,24576]{2,1,0:T(1,128)S(1)}, u32[]{:S(2)}, u32[]{:S(2)}) async-start(f32[8,1,24576]{2,1,0:T(1,128)} %reshape.298), calls=%async_computation.1 | async-start | bytes 1572864 | tf_op jit(solution)/shard_map/all_to_all | solution.py:156
  122.4 11.0 %copy-start.2 = (f32[64,32,256]{2,1,0:T(8,128)S(1)}, f32[64,32,256]{2,1,0:T(8,128)}, u32[]{:S(2)}) copy-start(f32[64,32,256]{2,1,0:T(8,128)} %param.3) | copy-start | bytes 6291460
  128.0 25.4 %all-to-all-start.2 = ((f32[8,1,24576]{2,1,0:T(1,128)}), f32[8,1,24576]{2,1,0:T(1,128)}, u32[]{:S(2)}, u32[]{:S(2)}) async-start(f32[8,1,24576]{2,1,0:T(1,128)} %reshape.300), calls=%async_computation.2 | async-start | bytes 1572864 | tf_op jit(solution)/shard_map/all_to_all | solution.py:179
  191.2 14.6 %all-to-all-start.3 = ((f32[4,1,49152]{2,1,0:T(1,128)}), f32[4,1,49152]{2,1,0:T(1,128)}, u32[]{:S(2)}, u32[]{:S(2)}) async-start(f32[4,1,49152]{2,1,0:T(1,128)} %reshape.302), calls=%async_computation.3 | async-start | bytes 1572864 | tf_op jit(solution)/shard_map/all_to_all | solution.py:185
  233.5 3.6 collective-permute-start
  234.3 2.8 collective-permute-start.1
  238.2 69.7 %collective-permute-start.2 = (f32[3,34,1,128]{3,1,0,2:T(8,128)S(1)}, f32[3,34,1,128]{3,1,0,2:T(8,128)S(1)}, u32[]{:S(2)}, u32[]{:S(2)}) collective-permute-start(f32[3,34,1,128]{3,1,0,2:T(8,128)S(1)} %get-tuple-element.60), channel_id=1, source_target_pairs={{0,1},{1,2},{2,3},{3,4},{4,5},{5,6},{6,7},{7,0},{8,9},{9,10},{10,1... | collective-permute-start | bytes 156680 | tf_op jit(solution)/shard_map/ppermute | solution.py:19
  240.0 68.0 %collective-permute-start.3 = (f32[3,34,1,128]{3,1,0,2:T(8,128)S(1)}, f32[3,34,1,128]{3,1,0,2:T(8,128)S(1)}, u32[]{:S(2)}, u32[]{:S(2)}) collective-permute-start(f32[3,34,1,128]{3,1,0,2:T(8,128)S(1)} %get-tuple-element.61), channel_id=1, source_target_pairs={{1,0},{2,1},{3,2},{4,3},{5,4},{6,5},{7,6},{0,7},{9,8},{10,9},{11,1... | collective-permute-start | bytes 156680 | tf_op jit(solution)/shard_map/ppermute | solution.py:21
  262.1 3.2 copy-start.21
  371.5 6.2 %copy-start.19 = (f32[64,32,2]{2,0,1:T(8,128)S(1)}, f32[64,32,2]{2,0,1:T(8,128)}, u32[]{:S(2)}) copy-start(f32[64,32,2]{2,0,1:T(8,128)} %copy.350) | copy-start | bytes 49156
  371.5 6.2 %copy-start.20 = (f32[64,32,3]{2,0,1:T(8,128)S(1)}, f32[64,32,3]{2,0,1:T(8,128)}, u32[]{:S(2)}) copy-start(f32[64,32,3]{2,0,1:T(8,128)} %copy.352) | copy-start | bytes 73732
  372.2 5.5 %copy-start.15 = (f32[64,32,3]{2,0,1:T(8,128)S(1)}, f32[64,32,3]{2,0,1:T(8,128)}, u32[]{:S(2)}) copy-start(f32[64,32,3]{2,0,1:T(8,128)} %copy.341) | copy-start | bytes 73732
  372.2 5.5 %copy-start.16 = (f32[64,32,2]{2,0,1:T(8,128)S(1)}, f32[64,32,2]{2,0,1:T(8,128)}, u32[]{:S(2)}) copy-start(f32[64,32,2]{2,0,1:T(8,128)} %copy.343) | copy-start | bytes 49156
  372.2 5.5 %copy-start.17 = (f32[64,32,1]{2,0,1:T(8,128)S(1)}, f32[64,32,1]{2,0,1:T(8,128)}, u32[]{:S(2)}) copy-start(f32[64,32,1]{2,0,1:T(8,128)} %copy.345) | copy-start | bytes 24580
  372.3 5.5 %copy-start.18 = (f32[64,32,1]{2,0,1:T(8,128)S(1)}, f32[64,32,1]{2,0,1:T(8,128)}, u32[]{:S(2)}) copy-start(f32[64,32,1]{2,0,1:T(8,128)} %copy.348) | copy-start | bytes 24580
  374.0 3.7 copy-start.13
  374.0 3.8 copy-start.14
  375.7 3.6 copy-start.12
  377.4 3.0 copy-start.10
  404.4 7.5 %collective-permute-start.4 = (f32[2,3,32,256]{3,1,2,0:T(4,128)S(1)}, f32[2,3,32,256]{3,1,2,0:T(4,128)S(1)}, u32[]{:S(2)}, u32[]{:S(2)}) collective-permute-start(f32[2,3,32,256]{3,1,2,0:T(4,128)S(1)} %get-tuple-element.22), channel_id=1, source_target_pairs={{8,0},{16,8},{24,16},{0,24},{9,1},{17,9},{25,17},{1,25},{10,2},{18... | collective-permute-start | bytes 589832 | tf_op jit(solution)/shard_map/ppermute | solution.py:21
  406.5 11.8 %collective-permute-start.5 = (f32[2,3,32,256]{3,1,2,0:T(4,128)S(1)}, f32[2,3,32,256]{3,1,2,0:T(4,128)S(1)}, u32[]{:S(2)}, u32[]{:S(2)}) collective-permute-start(f32[2,3,32,256]{3,1,2,0:T(4,128)S(1)} %get-tuple-element.23), channel_id=1, source_target_pairs={{0,8},{8,16},{16,24},{24,0},{1,9},{9,17},{17,25},{25,1},{2,10},{10... | collective-permute-start | bytes 589832 | tf_op jit(solution)/shard_map/ppermute | solution.py:19
  440.2 12.5 %collective-permute-start.6 = (f32[2,64,3,256]{3,1,2,0:T(8,128)S(1)}, f32[2,64,3,256]{3,1,2,0:T(8,128)S(1)}, u32[]{:S(2)}, u32[]{:S(2)}) collective-permute-start(f32[2,64,3,256]{3,1,2,0:T(8,128)S(1)} %get-tuple-element.18), channel_id=1, source_target_pairs={{0,1},{1,2},{2,3},{3,4},{4,5},{5,6},{6,7},{7,0},{8,9},{9,10},{10,1... | collective-permute-start | bytes 1179656 | tf_op jit(solution)/shard_map/ppermute | solution.py:19
  445.0 10.4 %collective-permute-start.7 = (f32[2,64,3,256]{3,1,2,0:T(8,128)S(1)}, f32[2,64,3,256]{3,1,2,0:T(8,128)S(1)}, u32[]{:S(2)}, u32[]{:S(2)}) collective-permute-start(f32[2,64,3,256]{3,1,2,0:T(8,128)S(1)} %get-tuple-element.19), channel_id=1, source_target_pairs={{1,0},{2,1},{3,2},{4,3},{5,4},{6,5},{7,6},{0,7},{9,8},{10,9},{11,1... | collective-permute-start | bytes 1179656 | tf_op jit(solution)/shard_map/ppermute | solution.py:21
  456.3 21.6 %copy-start.1 = (f32[3,32,16,128]{3,2,1,0:T(8,128)S(1)}, f32[3,32,16,128]{3,2,1,0:T(8,128)}, u32[]{:S(2)}) copy-start(f32[3,32,16,128]{3,2,1,0:T(8,128)} %param.2) | copy-start | bytes 2359300
  (11 other events, 25.1 us)
where the time goes:
time: 483 us; the launch traced here: 478 us
  local copies, waits for them, and re-layouts  199 us (41%)
  other arithmetic  115 us (24%)
  waiting for transfers between devices  62.5 us (13%)
  blocking collectives  54.6 us (11%)
  starting transfers between devices  29.4 us (6%)
  matrix products  16 us (3%)
    unnamed x69, local copies, waits for them, and re-layouts  66.4 us
    pmax x1, blocking collectives, shards(): velocity_peak = lax.pmax(jnp.max(jnp.abs(velocity)), ('row', 'col'))  40.1 us
    add x2, other arithmetic, remesh_rim(): summed = summed + values * kernel_weight(offset - moved)  39.3 us
    another operation x3, other arithmetic, refine_rim(): jnp.stack([lower, upper], axis=grid_axis + 1)  29.5 us
    another operation x1, other arithmetic, shards(): rows_input = jnp.stack([swept, displaced[1]])  23.9 us
    all_to_all x1, waiting for transfers between devices, shards(): lax.all_to_all(spectrum, 'col', split_axis=4, concat_axis=2, tiled=True)  19.6 us
    another operation x3, local copies, waits for them, and re-layouts, rotate(): jnp.stack([real_cos - direction * imag_sin, imag_cos + direction * real_s...  18.6 us
    ppermute x4, waiting for transfers between devices, with_halo(): lax.ppermute(tail, axis, [(i, (i + 1) % count) for i in range(count)])  14.8 us
  transfers between devices with their start and end apart: 11, of which 8 were waited for; matrix products, arithmetic and copies ran while one was open for 8% of the time, Pallas kernels for 0%

commit v1 on v0

--- a/solution.py
+++ b/solution.py
@@ -7,6 +7,22 @@
 COURANT = 0.9
 EPSILON = 1e-06
 HIGHEST = lax.Precision.HIGHEST
+
+
+def exchange_in_pairs(array, axis, split, join):
+    ways, here = (lax.axis_size(axis), lax.axis_index(axis))
+    width = array.shape[split] // ways
+    shape = list(array.shape)
+    shape[split] = width
+    height = shape[join]
+    shape[join] = height * ways
+    full = jnp.zeros(shape, array.dtype)
+    for mask in range(ways):
+        part = lax.dynamic_slice_in_dim(array, (here ^ mask) * width, width, axis=split)
+        if mask:
+            part = lax.ppermute(part, axis, [(d, d ^ mask) for d in range(ways)])
+        full = lax.dynamic_update_slice_in_dim(full, part, (here ^ mask) * height, axis=join)
+    return full
 
 
 def with_halo(cells, sides, width):
@@ -153,11 +169,7 @@
         -1.0,
     )
     spectrum = rotate(
-        lax.all_to_all(spectrum, "col", split_axis=4, concat_axis=2, tiled=True),
-        "czkq,zw->ckqw",
-        cos_full,
-        sin_full,
-        -1.0,
+        exchange_in_pairs(spectrum, "col", 4, 2), "czkq,zw->ckqw", cos_full, sin_full, -1.0
     )
     first_count = spectrum.shape[2]
     second_count = spectrum.shape[3]

time: 483 us -> 647 us (1.34)
  local copies, waits for them, and re-layouts: 199 us -> 335 us
  waiting for transfers between devices: 62.5 us -> 95.5 us
  blocking collectives: 54.6 us -> 40.1 us
  starting transfers between devices: 29.4 us -> 37.4 us
    dynamic_update_slice x0 -> x8, local copies, waits for them, and re-layouts: none -> 162 us  [exchange_in_pairs(): lax.dynamic_update_slice_in_dim(full, part, (here ^ mask) * height, axis=...]
    ppermute x0 -> x7, waiting for transfers between devices: none -> 42.8 us  [exchange_in_pairs(): part = lax.ppermute(part, axis, [(d, d ^ mask) for d in range(ways)])]
    all_to_all x1 -> x0, blocking collectives: 14.5 us -> none  [shards(): lax.all_to_all(forward, 'row', split_axis=4, concat_axis=2, tiled=True)]
    ppermute x0 -> x7, starting transfers between devices: none -> 11.5 us  [exchange_in_pairs(): part = lax.ppermute(part, axis, [(d, d ^ mask) for d in range(ways)])]
    all_to_all x1, waiting for transfers between devices: 19.6 us -> 9.71 us  [shards(): lax.all_to_all(forward, 'row', split_axis=4, concat_axis=2, tiled=True)]
    unnamed x69 -> x71, local copies, waits for them, and re-layouts: 66.4 us -> 57.2 us
    ppermute x0 -> x7, local copies, waits for them, and re-layouts: none -> 9.08 us  [exchange_in_pairs(): part = lax.ppermute(part, axis, [(d, d ^ mask) for d in range(ways)])]
    all_to_all x1 -> x0, local copies, waits for them, and re-layouts: 8.02 us -> none  [shards(): lax.all_to_all(spectrum, 'col', split_axis=4, concat_axis=2, tiled=True)]
  transfers between devices with their start and end apart: 11 -> 18, of which waited for: 8 -> 9; matrix products, arithmetic and copies ran while one was open for 8% -> 29% of each run, Pallas kernels for 0% -> 0%
where the time goes in v1:
time: 647 us; the launch traced here: 643 us
  local copies, waits for them, and re-layouts  335 us (52%)
  other arithmetic  117 us (18%)
  waiting for transfers between devices  95.5 us (15%)
  blocking collectives  40.1 us (6%)
  starting transfers between devices  37.4 us (6%)
  matrix products  16 us (2%)
    dynamic_update_slice x8, local copies, waits for them, and re-layouts, exchange_in_pairs(): lax.dynamic_update_slice_in_dim(full, part, (here ^ mask) * height, axis=...  162 us
    unnamed x71, local copies, waits for them, and re-layouts  57.2 us
    ppermute x7, waiting for transfers between devices, exchange_in_pairs(): part = lax.ppermute(part, axis, [(d, d ^ mask) for d in range(ways)])  42.8 us
    pmax x1, blocking collectives, shards(): velocity_peak = lax.pmax(jnp.max(jnp.abs(velocity)), ('row', 'col'))  40.1 us
    add x2, other arithmetic, remesh_rim(): summed = summed + values * kernel_weight(offset - moved)  39.3 us
    another operation x3, other arithmetic, refine_rim(): jnp.stack([lower, upper], axis=grid_axis + 1)  29.2 us
    another operation x1, other arithmetic, shards(): rows_input = jnp.stack([swept, displaced[1]])  24 us
    ppermute x4, waiting for transfers between devices, with_halo(): lax.ppermute(tail, axis, [(i, (i + 1) % count) for i in range(count)])  14.8 us
  transfers between devices with their start and end apart: 18, of which 9 were waited for; matrix products, arithmetic and copies ran while one was open for 29% of the time, Pallas kernels for 0%

profile of v1, /device:TPU:1, one launch (start us, length us, event | category | flops | bytes accessed | tf_op | source)
XLA Modules:
  0.0 642.6 jit_solution(1982547323373641452)
XLA Ops:
  15.0 9.7 %all-to-all-done = f32[4,1,49152]{2,1,0:T(1,128)S(1)} async-done(((f32[4,1,49152]{2,1,0:T(1,128)}), f32[4,1,49152]{2,1,0:T(1,128)S(1)}, u32[]{:S(2)}, u32[]{:S(2)}) %all-to-all-start) | async-done | bytes 786464 | tf_op jit(solution)/shard_map/all_to_all | solution.py:165
  59.8 42.7 %collective-permute-done.1 = f32[2,3,16,16,16]{4,3,2,1,0:T(8,128)S(1)} collective-permute-done((f32[2,3,16,16,16]{4,3,2,1,0:T(8,128)S(1)}, f32[2,3,16,16,16]{4,3,2,1,0:T(8,128)S(1)}, u32[]{:S(2)}, u32[]{:S(2)}) %collective-permute-start.1) | collective-permute-done | bytes 98336 | tf_op jit(solution)/shard_map/ppermute | solution.py:23
  105.3 21.8 %dynamic_update_slice.24 = f32[2,3,128,16,16]{2,4,3,1,0:T(8,128)S(1)} dynamic-update-slice(f32[2,3,128,16,16]{2,4,3,1,0:T(8,128)S(1)} %broadcast_in_dim.53, f32[2,3,16,16,16]{2,4,3,1,0:T(8,128)S(1)} %copy.332, s32[]{:T(128)} %constant.301.clone.1, s32[]{:T(128)} %constant.301.clone.1, s32[]{:T(128)S(6)} %select_n.350, s32[]{:T(128)} %constant.301.clone.1, s32[]{:T(128)} %constant.301.clone.1) | dynamic-update-slice | bytes 196612 | tf_op jit(solution)/shard_map/dynamic_update_slice | solution.py:24
  128.6 9.3 %dynamic_update_slice.25 = f32[2,3,128,16,16]{2,4,3,1,0:T(8,128)S(1)} dynamic-update-slice(f32[2,3,128,16,16]{2,4,3,1,0:T(8,128)S(1)} %dynamic_update_slice.24, f32[2,3,16,16,16]{2,4,3,1,0:T(8,128)S(1)} %copy.333, s32[]{:T(128)} %constant.301.clone.1, s32[]{:T(128)} %constant.301.clone.1, s32[]{:T(128)S(6)} %select_n.351, s32[]{:T(128)} %constant.301.clone.1, s32[]{:T(128)} %constant.301.clone.1) | dynamic-update-slice | bytes 196612 | tf_op jit(solution)/shard_map/dynamic_update_slice | solution.py:24
  138.3 21.8 %dynamic_update_slice.26 = f32[2,3,128,16,16]{2,4,3,1,0:T(8,128)S(1)} dynamic-update-slice(f32[2,3,128,16,16]{2,4,3,1,0:T(8,128)S(1)} %dynamic_update_slice.25, f32[2,3,16,16,16]{2,4,3,1,0:T(8,128)S(1)} %copy.334, s32[]{:T(128)} %constant.301.clone.1, s32[]{:T(128)} %constant.301.clone.1, s32[]{:T(128)S(6)} %select_n.352, s32[]{:T(128)} %constant.301.clone.1, s32[]{:T(128)} %constant.301.clone.1) | dynamic-update-slice | bytes 196612 | tf_op jit(solution)/shard_map/dynamic_update_slice | solution.py:24
  161.5 21.8 %dynamic_update_slice.27 = f32[2,3,128,16,16]{2,4,3,1,0:T(8,128)S(1)} dynamic-update-slice(f32[2,3,128,16,16]{2,4,3,1,0:T(8,128)S(1)} %dynamic_update_slice.26, f32[2,3,16,16,16]{2,4,3,1,0:T(8,128)S(1)} %copy.335, s32[]{:T(128)} %constant.301.clone.1, s32[]{:T(128)} %constant.301.clone.1, s32[]{:T(128)S(6)} %select_n.353, s32[]{:T(128)} %constant.301.clone.1, s32[]{:T(128)} %constant.301.clone.1) | dynamic-update-slice | bytes 196612 | tf_op jit(solution)/shard_map/dynamic_update_slice | solution.py:24
  184.8 21.8 %dynamic_update_slice.28 = f32[2,3,128,16,16]{2,4,3,1,0:T(8,128)S(1)} dynamic-update-slice(f32[2,3,128,16,16]{2,4,3,1,0:T(8,128)S(1)} %dynamic_update_slice.27, f32[2,3,16,16,16]{2,4,3,1,0:T(8,128)S(1)} %copy.336, s32[]{:T(128)} %constant.301.clone.1, s32[]{:T(128)} %constant.301.clone.1, s32[]{:T(128)S(6)} %select_n.354, s32[]{:T(128)} %constant.301.clone.1, s32[]{:T(128)} %constant.301.clone.1) | dynamic-update-slice | bytes 196612 | tf_op jit(solution)/shard_map/dynamic_update_slice | solution.py:24
  208.0 21.8 %dynamic_update_slice.29 = f32[2,3,128,16,16]{2,4,3,1,0:T(8,128)S(1)} dynamic-update-slice(f32[2,3,128,16,16]{2,4,3,1,0:T(8,128)S(1)} %dynamic_update_slice.28, f32[2,3,16,16,16]{2,4,3,1,0:T(8,128)S(1)} %copy.337, s32[]{:T(128)} %constant.301.clone.1, s32[]{:T(128)} %constant.301.clone.1, s32[]{:T(128)S(6)} %select_n.355, s32[]{:T(128)} %constant.301.clone.1, s32[]{:T(128)} %constant.301.clone.1) | dynamic-update-slice | bytes 196612 | tf_op jit(solution)/shard_map/dynamic_update_slice | solution.py:24
  231.3 21.8 %dynamic_update_slice.30 = f32[2,3,128,16,16]{2,4,3,1,0:T(8,128)S(1)} dynamic-update-slice(f32[2,3,128,16,16]{2,4,3,1,0:T(8,128)S(1)} %dynamic_update_slice.29, f32[2,3,16,16,16]{2,4,3,1,0:T(8,128)S(1)} %copy.338, s32[]{:T(128)} %constant.301.clone.1, s32[]{:T(128)} %constant.301.clone.1, s32[]{:T(128)S(6)} %select_n.356, s32[]{:T(128)} %constant.301.clone.1, s32[]{:T(128)} %constant.301.clone.1) | dynamic-update-slice | bytes 196612 | tf_op jit(solution)/shard_map/dynamic_update_slice | solution.py:24
  254.5 22.0 %dynamic_update_slice.31 = f32[2,3,128,16,16]{2,4,3,1,0:T(8,128)S(1)} dynamic-update-slice(f32[2,3,128,16,16]{2,4,3,1,0:T(8,128)S(1)} %dynamic_update_slice.30, f32[2,3,16,16,16]{2,4,3,1,0:T(8,128)S(1)} %copy.339, s32[]{:T(128)} %constant.301.clone.1, s32[]{:T(128)} %constant.301.clone.1, s32[]{:T(128)S(6)} %select_n.357, s32[]{:T(128)} %constant.301.clone.1, s32[]{:T(128)} %constant.301.clone.1) | dynamic-update-slice | bytes 196612 | tf_op jit(solution)/shard_map/dynamic_update_slice | solution.py:24
  304.0 14.4 %all-to-all-done.1 = f32[8,1,24576]{2,1,0:T(1,128)} async-done(((f32[8,1,24576]{2,1,0:T(1,128)}), f32[8,1,24576]{2,1,0:T(1,128)}, u32[]{:S(2)}, u32[]{:S(2)}) %all-to-all-start.1) | async-done | bytes 786464 | tf_op jit(solution)/shard_map/all_to_all | solution.py:191
  326.8 6.4 copy.395
  364.5 6.0 all-to-all-done.2
  379.3 6.7 %copy.343 = f32[2,3,16,16,4,32]{5,3,2,4,1,0:T(8,128)} copy(f32[2,3,16,16,4,32]{3,2,1,0,5,4:T(8,128)} %bitcast.175) | data formatting | bytes 1572864 | tf_op jit(solution)/shard_map/all_to_all | solution.py:197
  431.9 40.1 %pmax.7 = f32[]{:T(128)} all-reduce(f32[]{:T(128)} %get-tuple-element.5), channel_id=1, replica_groups=mesh['row'=4,'col'=8] {'row','col'}, use_global_device_ids=true, to_apply=%region_1.2 | all-reduce | flops 1 | bytes 8 | tf_op jit(solution)/shard_map/pmax | solution.py:201
  476.8 9.8 %copy.352 = f32[3,34,18,128,2]{1,4,3,2,0:T(2,128)} copy(f32[3,34,18,128,2]{3,1,2,0,4:T(8,128)} %pad_maximum_fusion.3) | data formatting | bytes 3760128 | tf_op jit(solution)/shard_map/stack | solution.py:115
  486.6 11.8 %fusion.3 = (f32[3,32,1,18,256]{1,4,3,0,2:T(8,128)}, f32[3,32,1,18,256]{1,4,3,0,2:T(8,128)}) fusion(f32[3,34,18,256]{1,3,2,0:T(8,128)} %bitcast.167), kind=kLoop, calls=%fused_computation.6 | loop fusion | flops 2211840 | bytes 8847360 | tf_op jit(solution)/shard_map/stack | solution.py:125
  498.4 12.6 %pad_maximum_fusion = f32[3,32,2,18,256]{1,4,3,0,2:T(8,128)} fusion(f32[3,32,1,18,256]{1,4,3,0,2:T(8,128)} %get-tuple-element.8, f32[3,32,1,18,256]{1,4,3,0,2:T(8,128)} %get-tuple-element.7), kind=kLoop, calls=%fused_computation | loop fusion | flops 884736 | bytes 7077888 | tf_op jit(solution)/shard_map/stack | solution.py:125
  511.0 10.9 %copy.353 = f32[3,32,2,18,256]{4,2,1,3,0:T(2,128)} copy(f32[3,32,2,18,256]{1,4,3,0,2:T(8,128)} %pad_maximum_fusion) | data formatting | bytes 7077888 | tf_op jit(solution)/shard_map/stack | solution.py:125
  544.9 24.0 %fusion.21 = f32[1,64,32,256]{3,1,2,0:T(8,128)S(1)} fusion(f32[64,32,3]{2,0,1:T(8,128)S(1)} %copy-done.15, f32[64,32,253]{2,0,1:T(8,128)S(1)} %copy-done.9, f32[64,32,2]{2,0,1:T(8,128)S(1)} %copy-done.16, f32[64,32,254]{2,0,1:T(8,128)S(1)} %copy-done.10, f32[64,32,1]{2,0,1:T(8,128)S(1)} %copy-done.17, f32[64,32,255]{2,0,1:T(8,128)S(1)} %copy-done.11, ...), kind=kLoop, calls=%fused_computation.57 | loop fusion | flops 152567808 | bytes 31457280 | tf_op jit(solution)/shard_map/stack | solution.py:208
  576.6 6.3 collective-permute-done.12
  584.4 20.3 %fusion.76 = f32[1,64,32,256]{3,1,2,0:T(8,128)S(1)} fusion(f32[1,64,32,256]{3,1,2,0:T(8,128)S(1)} %fusion.21, f32[2,67,32,256]{3,1,2,0:T(8,128)S(1)} %get-tuple-element.19, f32[2,67,32,256]{3,1,2,0:T(8,128)S(1)} %get-tuple-element.18, f32[1,64,32,256]{3,1,2,0:T(8,128)S(1)} %bitcast.170), kind=kLoop, calls=%fused_computation.112 | loop fusion | flops 146276352 | bytes 31457280 | tf_op jit(solution)/shard_map/add | solution.py:145
  609.6 7.7 %collective-permute-done.13 = f32[2,64,3,256]{3,1,2,0:T(8,128)S(1)} collective-permute-done((f32[2,64,3,256]{3,1,2,0:T(8,128)S(1)}, f32[2,64,3,256]{3,1,2,0:T(8,128)S(1)}, u32[]{:S(2)}, u32[]{:S(2)}) %collective-permute-start.13) | collective-permute-done | bytes 393248 | tf_op jit(solution)/shard_map/ppermute | solution.py:35
  620.9 19.0 %fusion.131 = f32[64,32,256]{2,0,1:T(8,128)S(1)} fusion(f32[64,38,256]{2,0,1:T(8,128)S(1)} %get-tuple-element.15, f32[64,38,256]{2,0,1:T(8,128)S(1)} %get-tuple-element.14), kind=kLoop, calls=%fused_computation.167 | loop fusion | flops 146276352 | bytes 31457280 | tf_op jit(solution)/shard_map/add | solution.py:145
  (200 shorter events, 230.5 us)
Async XLA Ops:
  10.1 14.6 %all-to-all-start = ((f32[4,1,49152]{2,1,0:T(1,128)}), f32[4,1,49152]{2,1,0:T(1,128)S(1)}, u32[]{:S(2)}, u32[]{:S(2)}) async-start(f32[4,1,49152]{2,1,0:T(1,128)} %reshape.292), calls=%async_computation | async-start | bytes 1572864 | tf_op jit(solution)/shard_map/all_to_all | solution.py:165
  49.0 7.5 %collective-permute-start = (f32[2,3,16,16,16]{4,3,2,1,0:T(8,128)S(1)}, f32[2,3,16,16,16]{4,3,2,1,0:T(8,128)S(1)}, u32[]{:S(2)}, u32[]{:S(2)}) collective-permute-start(f32[2,3,16,16,16]{4,3,2,1,0:T(8,128)S(1)} %get-tuple-element.66), channel_id=1, source_target_pairs={{0,1},{1,0},{2,3},{3,2},{4,5},{5,4},{6,7},{7,6},{8,9},{9,8},{10,11... | collective-permute-start | bytes 294920 | tf_op jit(solution)/shard_map/ppermute | solution.py:23
  50.4 52.1 %collective-permute-start.1 = (f32[2,3,16,16,16]{4,3,2,1,0:T(8,128)S(1)}, f32[2,3,16,16,16]{4,3,2,1,0:T(8,128)S(1)}, u32[]{:S(2)}, u32[]{:S(2)}) collective-permute-start(f32[2,3,16,16,16]{4,3,2,1,0:T(8,128)S(1)} %get-tuple-element.67), channel_id=1, source_target_pairs={{0,2},{1,3},{2,0},{3,1},{4,6},{5,7},{6,4},{7,5},{8,10},{9,11},{10,... | collective-permute-start | bytes 294920 | tf_op jit(solution)/shard_map/ppermute | solution.py:23
  51.8 108.3 %collective-permute-start.2 = (f32[2,3,16,16,16]{4,3,2,1,0:T(8,128)}, f32[2,3,16,16,16]{4,3,2,1,0:T(8,128)}, u32[]{:S(2)}, u32[]{:S(2)}) collective-permute-start(f32[2,3,16,16,16]{4,3,2,1,0:T(8,128)} %get-tuple-element.68), channel_id=1, source_target_pairs={{0,3},{1,2},{2,1},{3,0},{4,7},{5,6},{6,5},{7,4},{8,11},{9,10},{10,... | collective-permute-start | bytes 294920 | tf_op jit(solution)/shard_map/ppermute | solution.py:23
  52.1 131.2 %collective-permute-start.3 = (f32[2,3,16,16,16]{4,3,2,1,0:T(8,128)}, f32[2,3,16,16,16]{4,3,2,1,0:T(8,128)}, u32[]{:S(2)}, u32[]{:S(2)}) collective-permute-start(f32[2,3,16,16,16]{4,3,2,1,0:T(8,128)} %get-tuple-element.69), channel_id=1, source_target_pairs={{0,4},{1,5},{2,6},{3,7},{4,0},{5,1},{6,2},{7,3},{8,12},{9,13},{10,... | collective-permute-start | bytes 294920 | tf_op jit(solution)/shard_map/ppermute | solution.py:23
  56.1 150.5 %collective-permute-start.4 = (f32[2,3,16,16,16]{4,3,2,1,0:T(8,128)}, f32[2,3,16,16,16]{4,3,2,1,0:T(8,128)}, u32[]{:S(2)}, u32[]{:S(2)}) collective-permute-start(f32[2,3,16,16,16]{4,3,2,1,0:T(8,128)} %get-tuple-element.71), channel_id=1, source_target_pairs={{0,5},{1,4},{2,7},{3,6},{4,1},{5,0},{6,3},{7,2},{8,13},{9,12},{10,... | collective-permute-start | bytes 294920 | tf_op jit(solution)/shard_map/ppermute | solution.py:23
  56.5 48.4 %copy-start.25 = (f32[2,3,16,16,16]{4,3,2,1,0:T(8,128)}, f32[2,3,16,16,16]{4,3,2,1,0:T(8,128)S(1)}, u32[]{:S(2)}) copy-start(f32[2,3,16,16,16]{4,3,2,1,0:T(8,128)S(1)} %collective-permute-done) | copy-start | bytes 294916
  56.5 173.3 %collective-permute-start.5 = (f32[2,3,16,16,16]{4,3,2,1,0:T(8,128)}, f32[2,3,16,16,16]{4,3,2,1,0:T(8,128)}, u32[]{:S(2)}, u32[]{:S(2)}) collective-permute-start(f32[2,3,16,16,16]{4,3,2,1,0:T(8,128)} %get-tuple-element.70), channel_id=1, source_target_pairs={{0,6},{1,7},{2,4},{3,5},{4,2},{5,3},{6,0},{7,1},{8,14},{9,15},{10,... | collective-permute-start | bytes 294920 | tf_op jit(solution)/shard_map/ppermute | solution.py:23
  102.6 150.5 %collective-permute-start.6 = (f32[2,3,16,16,16]{4,3,2,1,0:T(8,128)}, f32[2,3,16,16,16]{4,3,2,1,0:T(8,128)}, u32[]{:S(2)}, u32[]{:S(2)}) collective-permute-start(f32[2,3,16,16,16]{4,3,2,1,0:T(8,128)} %get-tuple-element.64), channel_id=1, source_target_pairs={{0,7},{1,6},{2,5},{3,4},{4,3},{5,2},{6,1},{7,0},{8,15},{9,14},{10,... | collective-permute-start | bytes 294920 | tf_op jit(solution)/shard_map/ppermute | solution.py:23
  105.3 32.6 %copy-start.24 = (f32[2,3,16,16,16]{4,3,2,1,0:T(8,128)S(1)}, f32[2,3,16,16,16]{4,3,2,1,0:T(8,128)}, u32[]{:S(2)}) copy-start(f32[2,3,16,16,16]{4,3,2,1,0:T(8,128)} %copy-done.23) | copy-start | bytes 294916
  288.4 10.0 %copy-start.2 = (f32[64,32,256]{2,1,0:T(8,128)S(1)}, f32[64,32,256]{2,1,0:T(8,128)}, u32[]{:S(2)}) copy-start(f32[64,32,256]{2,1,0:T(8,128)} %param.3) | copy-start | bytes 6291460
  294.1 24.3 %all-to-all-start.1 = ((f32[8,1,24576]{2,1,0:T(1,128)}), f32[8,1,24576]{2,1,0:T(1,128)}, u32[]{:S(2)}, u32[]{:S(2)}) async-start(f32[8,1,24576]{2,1,0:T(1,128)} %reshape.294), calls=%async_computation.1 | async-start | bytes 1572864 | tf_op jit(solution)/shard_map/all_to_all | solution.py:191
  355.9 14.6 %all-to-all-start.2 = ((f32[4,1,49152]{2,1,0:T(1,128)}), f32[4,1,49152]{2,1,0:T(1,128)}, u32[]{:S(2)}, u32[]{:S(2)}) async-start(f32[4,1,49152]{2,1,0:T(1,128)} %reshape.296), calls=%async_computation.2 | async-start | bytes 1572864 | tf_op jit(solution)/shard_map/all_to_all | solution.py:197
  398.2 3.6 collective-permute-start.7
  399.0 2.8 collective-permute-start.8
  403.0 69.8 %collective-permute-start.9 = (f32[3,34,1,128]{3,1,0,2:T(8,128)S(1)}, f32[3,34,1,128]{3,1,0,2:T(8,128)S(1)}, u32[]{:S(2)}, u32[]{:S(2)}) collective-permute-start(f32[3,34,1,128]{3,1,0,2:T(8,128)S(1)} %get-tuple-element.58), channel_id=1, source_target_pairs={{0,1},{1,2},{2,3},{3,4},{4,5},{5,6},{6,7},{7,0},{8,9},{9,10},{10,1... | collective-permute-start | bytes 156680 | tf_op jit(solution)/shard_map/ppermute | solution.py:35
  404.8 68.0 %collective-permute-start.10 = (f32[3,34,1,128]{3,1,0,2:T(8,128)S(1)}, f32[3,34,1,128]{3,1,0,2:T(8,128)S(1)}, u32[]{:S(2)}, u32[]{:S(2)}) collective-permute-start(f32[3,34,1,128]{3,1,0,2:T(8,128)S(1)} %get-tuple-element.59), channel_id=1, source_target_pairs={{1,0},{2,1},{3,2},{4,3},{5,4},{6,5},{7,6},{0,7},{9,8},{10,9},{11,1... | collective-permute-start | bytes 156680 | tf_op jit(solution)/shard_map/ppermute | solution.py:37
  535.9 6.2 copy-start.19
  536.6 5.4 copy-start.15
  569.0 7.6 %collective-permute-start.11 = (f32[2,3,32,256]{3,1,2,0:T(4,128)S(1)}, f32[2,3,32,256]{3,1,2,0:T(4,128)S(1)}, u32[]{:S(2)}, u32[]{:S(2)}) collective-permute-start(f32[2,3,32,256]{3,1,2,0:T(4,128)S(1)} %get-tuple-element.20), channel_id=1, source_target_pairs={{8,0},{16,8},{24,16},{0,24},{9,1},{17,9},{25,17},{1,25},{10,2},{18... | collective-permute-start | bytes 589832 | tf_op jit(solution)/shard_map/ppermute | solution.py:37
  571.1 11.8 %collective-permute-start.12 = (f32[2,3,32,256]{3,1,2,0:T(4,128)S(1)}, f32[2,3,32,256]{3,1,2,0:T(4,128)S(1)}, u32[]{:S(2)}, u32[]{:S(2)}) collective-permute-start(f32[2,3,32,256]{3,1,2,0:T(4,128)S(1)} %get-tuple-element.21), channel_id=1, source_target_pairs={{0,8},{8,16},{16,24},{24,0},{1,9},{9,17},{17,25},{25,1},{2,10},{10... | collective-permute-start | bytes 589832 | tf_op jit(solution)/shard_map/ppermute | solution.py:35
  604.8 12.5 %collective-permute-start.13 = (f32[2,64,3,256]{3,1,2,0:T(8,128)S(1)}, f32[2,64,3,256]{3,1,2,0:T(8,128)S(1)}, u32[]{:S(2)}, u32[]{:S(2)}) collective-permute-start(f32[2,64,3,256]{3,1,2,0:T(8,128)S(1)} %get-tuple-element.16), channel_id=1, source_target_pairs={{0,1},{1,2},{2,3},{3,4},{4,5},{5,6},{6,7},{7,0},{8,9},{9,10},{10,1... | collective-permute-start | bytes 1179656 | tf_op jit(solution)/shard_map/ppermute | solution.py:35
  609.6 10.4 %collective-permute-start.14 = (f32[2,64,3,256]{3,1,2,0:T(8,128)S(1)}, f32[2,64,3,256]{3,1,2,0:T(8,128)S(1)}, u32[]{:S(2)}, u32[]{:S(2)}) collective-permute-start(f32[2,64,3,256]{3,1,2,0:T(8,128)S(1)} %get-tuple-element.17), channel_id=1, source_target_pairs={{1,0},{2,1},{3,2},{4,3},{5,4},{6,5},{7,6},{0,7},{9,8},{10,9},{11,1... | collective-permute-start | bytes 1179656 | tf_op jit(solution)/shard_map/ppermute | solution.py:37
  620.9 21.6 %copy-start.1 = (f32[3,32,16,128]{3,2,1,0:T(8,128)S(1)}, f32[3,32,16,128]{3,2,1,0:T(8,128)}, u32[]{:S(2)}) copy-start(f32[3,32,16,128]{3,2,1,0:T(8,128)} %param.2) | copy-start | bytes 2359300
  (20 other events, 61.1 us)
